TPU v7x, 32 devices: a whole 2x2x4 slice. The times are simulated.
32 devices in a mesh: batch: 4 (over x, core), lat: 8 (over z, y).
Axes of the slice: x: 2, y: 2, z: 4, core: 2. Of those that a mesh axis runs over, the one named last changes fastest.
Arguments:
- predicted: bfloat16 [4, 73, 192, 1440], P('batch', None, 'lat'), may hold values from -64 to 64
- target: bfloat16 [4, 73, 192, 1440], P('batch', None, 'lat'), may hold values from -128 to 128
- legendre_basis: bfloat16 [192, 96, 720], P(None, ('batch', 'lat')), may hold values from -1 to 1
Outputs:
- spectra: float32 [2, 73, 720], replicated
- channel_loss: float32 [73], replicated
All inputs are finite; a program needn't handle non-finite values.
Results may differ from a plain program's by a relative error of at most 0.0003.
Values may be sent and summed in bfloat16 or wider, within the bound.
No kernel may reach another device: no remote copies, remote signals or barrier semaphores. Data moves between devices by JAX's collectives and lax.ppermute only.
A program may use at most 128 MiB of HBM per device.

v0:
```python
import math
import jax
import jax.numpy as jnp
from jax import lax
from jax.sharding import PartitionSpec as P


def fourier_table(lon_count, order_count):
    lon_ids = jnp.arange(lon_count, dtype=jnp.int32)
    order_ids = jnp.arange(order_count, dtype=jnp.int32)
    product_ids = lon_ids[:, None] * order_ids[None, :] % lon_count
    angles = 2.0 * math.pi / lon_count * product_ids.astype(jnp.float32)
    inv_root = 1.0 / math.sqrt(lon_count)
    return jnp.stack([jnp.cos(angles) * inv_root, -jnp.sin(angles) * inv_root], axis=1).astype(
        jnp.bfloat16
    )


def band_energy(fourier, basis_block, orders):
    coefficients = jnp.einsum(
        "fpmbcn,nml->fpmbcl", fourier, basis_block, preferred_element_type=jnp.float32
    )
    squares = jnp.sum(coefficients * coefficients, axis=1)
    weights = jnp.where(orders == 0, 1.0, 2.0).astype(jnp.float32)
    return jnp.sum(squares * weights[None, :, None, None, None], axis=(1, 2))


def body(predicted, target, legendre_basis):
    groups = lax.axis_size("batch")
    band_count = lax.axis_size("lat")
    per_dev = legendre_basis.shape[1]
    order_count = per_dev * groups * band_count
    dft_table = fourier_table(predicted.shape[3], order_count)
    band_id = lax.axis_index("lat")

    def transform(field_in):
        return jnp.einsum(
            "bcnk,kpm->pmbcn", field_in, dft_table, preferred_element_type=jnp.float32
        ).astype(jnp.bfloat16)

    fourier = jnp.stack([transform(predicted), transform(target)], axis=0)
    members = fourier.shape[3]
    channels = fourier.shape[4]
    lat_rows = fourier.shape[5]
    fourier = fourier.reshape(2, 2, groups, band_count, per_dev, members, channels, lat_rows)
    arrived = lax.all_to_all(fourier, "lat", split_axis=3, concat_axis=7, tiled=True)
    arrived = arrived.reshape(
        2, 2, groups * per_dev, arrived.shape[5], arrived.shape[6], arrived.shape[7]
    )
    basis_block = lax.all_gather(legendre_basis, "batch", axis=1, tiled=True)
    taken = basis_block.shape[1]
    gathered_ids = jnp.arange(taken, dtype=jnp.int32)
    orders = (
        gathered_ids // per_dev * band_count * per_dev + band_id * per_dev + gathered_ids % per_dev
    )
    partial_value = band_energy(arrived, basis_block, orders)
    energy = lax.psum(partial_value, "lat")
    energy = lax.psum(energy, "batch")
    spectra = energy / (predicted.shape[0] * groups * order_count)
    log_spectra = jnp.log(spectra + 1e-06)
    channel_loss = jnp.mean((log_spectra[0] - log_spectra[1]) ** 2, axis=1)
    return (spectra, channel_loss)


def solution(mesh):
    placed = (
        P("batch", None, "lat", None),
        P("batch", None, "lat", None),
        P(None, ("batch", "lat"), None),
    )
    return jax.shard_map(body, mesh=mesh, in_specs=placed, out_specs=(P(), P()), check_vma=False)
```

profile of v0, /device:TPU:0, one launch (start us, length us, event | category | flops | bytes accessed | tf_op | source)
XLA Modules:
  0.0 212.2 jit_solution(11625327290755649896)
XLA Ops:
  7.2 0.0 all-gather.2.cloned.1.call-start
  7.2 0.7 all-gather.2.cloned.1.call-update
  7.9 2.6 %multiply_convert_fusion = (bf16[1440,1,96]{0,2,1:T(8,128)(2,1)S(1)}, bf16[1440,1,96]{0,2,1:T(8,128)(2,1)S(1)}) fusion(), kind=kLoop, calls=%fused_computation.17 | loop fusion | flops 1935360 | bytes 552960 | tf_op jit(solution)/shard_map/convert.1
  10.5 0.0 copy-start
  10.5 0.0 copy-start.1
  10.5 0.7 copy-done
  11.2 0.1 copy-done.1
  11.3 4.8 %fusion.8 = bf16[2,96,73,24]{1,2,3,0:T(8,128)(2,1)S(1)} fusion(bf16[73,24,1440]{2,1,0:T(8,128)(2,1)} %bitcast.33, bf16[1440,1,96]{0,2,1:T(8,128)(2,1)S(1)} %get-tuple-element.4, bf16[1440,1,96]{0,2,1:T(8,128)(2,1)S(1)} %get-tuple-element.5), kind=kOutput, calls=%fused_computation.11 | convolution fusion | flops 970228224 | bytes 6271488 | tf_op jit(solution)/shard_map/bcnk,kpm->pmbcn/dot_general | solution.py:37
  16.1 0.9 copy.29
  17.0 5.5 %fusion.11 = bf16[2,96,73,24]{1,2,3,0:T(8,128)(2,1)S(1)} fusion(bf16[73,24,1440]{2,1,0:T(8,128)(2,1)} %bitcast.34, bf16[1440,1,96]{0,2,1:T(8,128)(2,1)} %copy-done, bf16[1440,1,96]{0,2,1:T(8,128)(2,1)} %copy-done.1), kind=kOutput, calls=%fused_computation.12 | convolution fusion | flops 970228224 | bytes 6271488 | tf_op jit(solution)/shard_map/bcnk,kpm->pmbcn/dot_general | solution.py:37
  22.5 0.9 copy.31
  23.3 0.5 pad_maximum_fusion
  23.9 2.0 copy.32
  25.9 7.5 %all-to-all-start = ((bf16[2,2,4,8,3,1,73,24]{6,7,4,2,1,5,0,3:T(8,128)(2,1)}), bf16[2,2,4,8,3,1,73,24]{6,7,4,2,1,5,0,3:T(8,128)(2,1)S(1)}, u32[]{:S(2)}, u32[]{:S(2)}) async-start(bf16[2,2,4,8,3,1,73,24]{6,7,4,2,1,5,0,3:T(8,128)(2,1)} %copy.32), calls=%async_computation | async-start | bytes 4718592 | tf_op jit(solution)/shard_map/all_to_all | solution.py:46
  33.5 0.0 all-reduce.3.cloned.1.call-start
  33.5 53.6 %all-to-all-done = bf16[2,2,4,8,3,1,73,24]{6,7,4,2,1,5,0,3:T(8,128)(2,1)S(1)} async-done(((bf16[2,2,4,8,3,1,73,24]{6,7,4,2,1,5,0,3:T(8,128)(2,1)}), bf16[2,2,4,8,3,1,73,24]{6,7,4,2,1,5,0,3:T(8,128)(2,1)S(1)}, u32[]{:S(2)}, u32[]{:S(2)}) %all-to-all-start) | async-done | bytes 1345568 | tf_op jit(solution)/shard_map/all_to_all | solution.py:46
  87.1 2.1 copy.33
  89.2 0.0 all-gather.2.cloned.1.call-done
  89.2 5.1 %multiply_reduce_fusion = f32[12,2,73,720]{3,2,1,0:T(8,128)S(1)} fusion(bf16[192,12,720]{2,0,1:T(8,128)(2,1)} %all-gather.2.cloned.1.call-done, bf16[2,2,12,73,192]{3,4,2,1,0:T(8,128)(2,1)} %bitcast.30), kind=kOutput, calls=%fused_computation | convolution fusion | flops 972570240 | bytes 9709056 | tf_op jit(solution)/shard_map/fpmbcn,nml->fpmbcl/dot_general | solution.py:20
  94.3 0.6 multiply_reduce_fusion.1
  94.9 1.1 copy.40
  96.0 0.0 all-reduce.3.cloned.1.call-update
  96.1 0.0 all-reduce.5.cloned.1.call-start
  96.1 71.4 %all-reduce.3.cloned.1.call-done = f32[2,73,720]{2,0,1:T(2,128)} async-done(((f32[2,73,720]{2,0,1:T(2,128)}), f32[2,73,720]{2,0,1:T(2,128)}) %all-reduce.3.cloned.1.call-update) | async-done | bytes 420496 | tf_op jit(solution)/shard_map/psum | solution.py:57
  167.5 0.0 all-reduce.5.cloned.1.call-update
  167.6 34.7 %all-reduce.5.cloned.1.call-done = f32[2,73,720]{2,0,1:T(2,128)} async-done(((f32[2,73,720]{2,0,1:T(2,128)}), f32[2,73,720]{2,0,1:T(2,128)}) %all-reduce.5.cloned.1.call-update) | async-done | bytes 420496 | tf_op jit(solution)/shard_map/psum | solution.py:58
  202.2 2.2 %add_log_fusion = (f32[2,73,720]{2,0,1:T(2,128)S(1)}, f32[2,73,720]{2,0,1:T(2,128)}) fusion(f32[2,73,720]{2,0,1:T(2,128)} %all-reduce.5.cloned.1.call-done), kind=kLoop, calls=%fused_computation.23 | loop fusion | flops 210240 | bytes 1261440 | tf_op jit(solution)/shard_map/log | solution.py:60
  204.5 0.6 fusion.20
  205.1 0.5 broadcast_multiply_fusion.1
  (1 shorter events, 0.0 us)
Async XLA Ops:
  7.2 82.1 %all-gather.2.cloned.1.call-start = ((), (), s32[]{:S(2)}) async-start(), calls=%async_computation.1 | async-start | bytes 4423680 | tf_op jit(solution)/shard_map/all_gather | solution.py:50
  10.5 0.7 copy-start
  10.5 0.8 copy-start.1
  25.9 61.2 %all-to-all-start = ((bf16[2,2,4,8,3,1,73,24]{6,7,4,2,1,5,0,3:T(8,128)(2,1)}), bf16[2,2,4,8,3,1,73,24]{6,7,4,2,1,5,0,3:T(8,128)(2,1)S(1)}, u32[]{:S(2)}, u32[]{:S(2)}) async-start(bf16[2,2,4,8,3,1,73,24]{6,7,4,2,1,5,0,3:T(8,128)(2,1)} %copy.32), calls=%async_computation | async-start | bytes 4718592 | tf_op jit(solution)/shard_map/all_to_all | solution.py:46
  33.5 134.1 %all-reduce.3.cloned.1.call-start = ((), (), s32[]{:S(2)}) async-start(), calls=%async_computation.2 | async-start | bytes 897024 | tf_op jit(solution)/shard_map/psum | solution.py:57
  96.1 106.2 %all-reduce.5.cloned.1.call-start = ((), (), s32[]{:S(2)}) async-start(), calls=%async_computation.3 | async-start | bytes 897024 | tf_op jit(solution)/shard_map/psum | solution.py:58
Sparse Core Ops, SparseCore 0:
  9.5 33.4 all-gather.1
  96.2 71.2 all-reduce.2
  169.9 32.2 all-reduce.4
where the time goes:
time: 212 us
  waiting for transfers between devices  160 us (75%)
  matrix products  15.4 us (7%)
  between operations  13.8 us (7%)
  local copies, waits for them, and re-layouts  7.77 us (4%)
  starting transfers between devices  7.66 us (4%)
  other arithmetic  7.07 us (3%)
    psum x1, waiting for transfers between devices, body(): energy = lax.psum(partial_value, 'lat')  71.4 us
    all_to_all x1, waiting for transfers between devices, body(): lax.all_to_all(fourier, 'lat', split_axis=3, concat_axis=7, tiled=True)  53.6 us
    psum x1, waiting for transfers between devices, body(): energy = lax.psum(energy, 'batch')  34.7 us
    dot_general x2, matrix products, transform(): jnp.einsum('bcnk,kpm->pmbcn', field_in, dft_table, preferred_element_type...  10.3 us
    all_to_all x1, starting transfers between devices, body(): lax.all_to_all(fourier, 'lat', split_axis=3, concat_axis=7, tiled=True)  7.55 us
    dot_general x1, matrix products, band_energy(): jnp.einsum('fpmbcn,nml->fpmbcl', fourier, basis_block, preferred_element_...  5.1 us
  transfers between devices with their start and end apart: 4, of which 3 were waited for; matrix products, arithmetic and copies ran while one was open for 9% of the time, Pallas kernels for 0%

commit v1 on v0

--- a/solution.py
+++ b/solution.py
@@ -55,7 +55,18 @@
     )
     partial_value = band_energy(arrived, basis_block, orders)
     energy = lax.psum(partial_value, "lat")
-    energy = lax.psum(energy, "batch")
+
+    def local_data_render(inner_x):
+        ndev = lax.psum(1, "batch")
+        item_now = inner_x
+        for q in [t for t in (1, 2, 4, 8, 16) if t < ndev]:
+            local_out = lax.ppermute(
+                item_now, "batch", list(map(lambda dev: (dev, dev ^ q), range(ndev)))
+            )
+            item_now = item_now + local_out
+        return item_now
+
+    energy = local_data_render(energy)
     spectra = energy / (predicted.shape[0] * groups * order_count)
     log_spectra = jnp.log(spectra + 1e-06)
     channel_loss = jnp.mean((log_spectra[0] - log_spectra[1]) ** 2, axis=1)

time: 212 us -> 193 us (0.910)
  waiting for transfers between devices: 160 us -> 138 us
    psum x1 -> x0, waiting for transfers between devices: 34.7 us -> none  [body(): energy = lax.psum(energy, 'batch')]
    ppermute x0 -> x2, waiting for transfers between devices: none -> 12.9 us  [local_data_render(): lax.ppermute(item_now, 'batch', list(map(lambda dev: (dev, dev ^ q), rang...]
  transfers between devices with their start and end apart: 4 -> 5, of which waited for: 3 -> 4; matrix products, arithmetic and copies ran while one was open for 9% -> 10% of each run, Pallas kernels for 0% -> 0%
where the time goes in v1:
time: 193 us; the launch traced here: 192 us
  waiting for transfers between devices  138 us (72%)
  matrix products  15.4 us (8%)
  between operations  14.1 us (7%)
  starting transfers between devices  9.33 us (5%)
  local copies, waits for them, and re-layouts  7.75 us (4%)
  other arithmetic  7.38 us (4%)
    psum x1, waiting for transfers between devices, body(): energy = lax.psum(partial_value, 'lat')  71.5 us
    all_to_all x1, waiting for transfers between devices, body(): lax.all_to_all(fourier, 'lat', split_axis=3, concat_axis=7, tiled=True)  53.4 us
    ppermute x2, waiting for transfers between devices, local_data_render(): lax.ppermute(item_now, 'batch', list(map(lambda dev: (dev, dev ^ q), rang...  12.9 us
    dot_general x2, matrix products, transform(): jnp.einsum('bcnk,kpm->pmbcn', field_in, dft_table, preferred_element_type...  10.3 us
    all_to_all x1, starting transfers between devices, body(): lax.all_to_all(fourier, 'lat', split_axis=3, concat_axis=7, tiled=True)  7.54 us
    dot_general x1, matrix products, band_energy(): jnp.einsum('fpmbcn,nml->fpmbcl', fourier, basis_block, preferred_element_...  5.1 us
  transfers between devices with their start and end apart: 5, of which 4 were waited for; matrix products, arithmetic and copies ran while one was open for 10% of the time, Pallas kernels for 0%

profile of v1, /device:TPU:0, one launch (start us, length us, event | category | flops | bytes accessed | tf_op | source)
XLA Modules:
  0.0 192.5 jit_solution(503882210114959273)
XLA Ops:
  7.2 0.0 all-gather.2.cloned.1.call-start
  7.2 0.7 all-gather.2.cloned.1.call-update
  7.9 2.6 %multiply_convert_fusion = (bf16[1440,1,96]{0,2,1:T(8,128)(2,1)S(1)}, bf16[1440,1,96]{0,2,1:T(8,128)(2,1)S(1)}) fusion(), kind=kLoop, calls=%fused_computation.17 | loop fusion | flops 1935360 | bytes 552960 | tf_op jit(solution)/shard_map/convert.1
  10.5 0.0 copy-start
  10.5 0.0 copy-start.1
  10.5 0.7 copy-done
  11.2 0.1 copy-done.1
  11.3 4.8 %fusion.8 = bf16[2,96,73,24]{1,2,3,0:T(8,128)(2,1)S(1)} fusion(bf16[73,24,1440]{2,1,0:T(8,128)(2,1)} %bitcast.33, bf16[1440,1,96]{0,2,1:T(8,128)(2,1)S(1)} %get-tuple-element.4, bf16[1440,1,96]{0,2,1:T(8,128)(2,1)S(1)} %get-tuple-element.5), kind=kOutput, calls=%fused_computation.11 | convolution fusion | flops 970228224 | bytes 6271488 | tf_op jit(solution)/shard_map/bcnk,kpm->pmbcn/dot_general | solution.py:37
  16.1 0.9 copy.29
  17.0 5.5 %fusion.11 = bf16[2,96,73,24]{1,2,3,0:T(8,128)(2,1)S(1)} fusion(bf16[73,24,1440]{2,1,0:T(8,128)(2,1)} %bitcast.34, bf16[1440,1,96]{0,2,1:T(8,128)(2,1)} %copy-done, bf16[1440,1,96]{0,2,1:T(8,128)(2,1)} %copy-done.1), kind=kOutput, calls=%fused_computation.12 | convolution fusion | flops 970228224 | bytes 6271488 | tf_op jit(solution)/shard_map/bcnk,kpm->pmbcn/dot_general | solution.py:37
  22.5 0.9 copy.31
  23.4 0.5 pad_maximum_fusion
  23.9 2.0 %copy.32 = bf16[2,2,4,8,3,1,73,24]{6,7,4,2,1,5,0,3:T(8,128)(2,1)} copy(bf16[2,2,4,8,3,1,73,24]{6,7,4,3,2,1,5,0:T(8,128)(2,1)S(1)} %pad_maximum_fusion) | data formatting | bytes 2691072 | tf_op jit(solution)/shard_map/stack | solution.py:41
  25.9 7.5 %all-to-all-start = ((bf16[2,2,4,8,3,1,73,24]{6,7,4,2,1,5,0,3:T(8,128)(2,1)}), bf16[2,2,4,8,3,1,73,24]{6,7,4,2,1,5,0,3:T(8,128)(2,1)S(1)}, u32[]{:S(2)}, u32[]{:S(2)}) async-start(bf16[2,2,4,8,3,1,73,24]{6,7,4,2,1,5,0,3:T(8,128)(2,1)} %copy.32), calls=%async_computation | async-start | bytes 4718592 | tf_op jit(solution)/shard_map/all_to_all | solution.py:46
  33.5 0.2 all-reduce.2.cloned.1.call-start
  33.7 53.4 %all-to-all-done = bf16[2,2,4,8,3,1,73,24]{6,7,4,2,1,5,0,3:T(8,128)(2,1)S(1)} async-done(((bf16[2,2,4,8,3,1,73,24]{6,7,4,2,1,5,0,3:T(8,128)(2,1)}), bf16[2,2,4,8,3,1,73,24]{6,7,4,2,1,5,0,3:T(8,128)(2,1)S(1)}, u32[]{:S(2)}, u32[]{:S(2)}) %all-to-all-start) | async-done | bytes 1345568 | tf_op jit(solution)/shard_map/all_to_all | solution.py:46
  87.1 2.1 %copy.33 = bf16[2,2,4,1,3,1,73,8,24]{6,8,7,4,2,1,0,5,3:T(8,128)(2,1)} copy(bf16[2,2,4,1,3,1,73,8,24]{6,8,4,2,1,0,7,5,3:T(8,128)(2,1)S(1)} %bitcast.29) | data formatting | bytes 2691072 | tf_op jit(solution)/shard_map/all_to_all | solution.py:46
  89.2 0.0 all-gather.2.cloned.1.call-done
  89.2 5.1 %multiply_reduce_fusion = f32[12,2,73,720]{3,2,1,0:T(8,128)S(1)} fusion(bf16[192,12,720]{2,0,1:T(8,128)(2,1)} %all-gather.2.cloned.1.call-done, bf16[2,2,12,73,192]{3,4,2,1,0:T(8,128)(2,1)} %bitcast.30), kind=kOutput, calls=%fused_computation | convolution fusion | flops 972570240 | bytes 9709056 | tf_op jit(solution)/shard_map/fpmbcn,nml->fpmbcl/dot_general | solution.py:20
  94.3 0.6 multiply_reduce_fusion.1
  94.9 1.1 copy.40
  96.0 0.0 all-reduce.2.cloned.1.call-update
  96.0 71.5 %all-reduce.2.cloned.1.call-done = f32[2,73,720]{2,0,1:T(2,128)} async-done(((f32[2,73,720]{2,0,1:T(2,128)}), f32[2,73,720]{2,0,1:T(2,128)}) %all-reduce.2.cloned.1.call-update) | async-done | bytes 420496 | tf_op jit(solution)/shard_map/psum | solution.py:57
  167.5 0.0 collective-permute-start
  167.5 2.0 %collective-permute-done = f32[2,73,720]{2,0,1:T(2,128)S(1)} collective-permute-done((f32[2,73,720]{2,0,1:T(2,128)}, f32[2,73,720]{2,0,1:T(2,128)S(1)}, u32[]{:S(2)}, u32[]{:S(2)}) %collective-permute-start) | collective-permute-done | bytes 420512 | tf_op jit(solution)/shard_map/ppermute | solution.py:63
  169.5 1.2 add.70
  170.8 1.5 collective-permute-start.1
  172.3 10.9 %collective-permute-done.1 = f32[2,73,720]{2,0,1:T(2,128)S(1)} collective-permute-done((f32[2,73,720]{2,0,1:T(2,128)S(1)}, f32[2,73,720]{2,0,1:T(2,128)S(1)}, u32[]{:S(2)}, u32[]{:S(2)}) %collective-permute-start.1) | collective-permute-done | bytes 420512 | tf_op jit(solution)/shard_map/ppermute | solution.py:63
  183.2 1.3 add_log_fusion
  184.5 0.6 fusion.20
  185.1 0.5 broadcast_multiply_fusion
  (1 shorter events, 0.0 us)
Async XLA Ops:
  7.2 82.1 %all-gather.2.cloned.1.call-start = ((), (), s32[]{:S(2)}) async-start(), calls=%async_computation.1 | async-start | bytes 4423680 | tf_op jit(solution)/shard_map/all_gather | solution.py:50
  10.5 0.7 copy-start
  10.5 0.8 copy-start.1
  25.9 61.2 %all-to-all-start = ((bf16[2,2,4,8,3,1,73,24]{6,7,4,2,1,5,0,3:T(8,128)(2,1)}), bf16[2,2,4,8,3,1,73,24]{6,7,4,2,1,5,0,3:T(8,128)(2,1)S(1)}, u32[]{:S(2)}, u32[]{:S(2)}) async-start(bf16[2,2,4,8,3,1,73,24]{6,7,4,2,1,5,0,3:T(8,128)(2,1)} %copy.32), calls=%async_computation | async-start | bytes 4718592 | tf_op jit(solution)/shard_map/all_to_all | solution.py:46
  33.5 134.1 %all-reduce.2.cloned.1.call-start = ((), (), s32[]{:S(2)}) async-start(), calls=%async_computation.2 | async-start | bytes 897024 | tf_op jit(solution)/shard_map/psum | solution.py:57
  167.5 2.0 %collective-permute-start = (f32[2,73,720]{2,0,1:T(2,128)}, f32[2,73,720]{2,0,1:T(2,128)S(1)}, u32[]{:S(2)}, u32[]{:S(2)}) collective-permute-start(f32[2,73,720]{2,0,1:T(2,128)} %all-reduce.2.cloned.1.call-done), channel_id=1, source_target_pairs={{0,8},{8,0},{16,24},{24,16},{1,9},{9,1},{17,25},{25,17},{2,10},{10... | collective-permute-start | bytes 1261448 | tf_op jit(solution)/shard_map/ppermute | solution.py:63
  170.8 12.4 %collective-permute-start.1 = (f32[2,73,720]{2,0,1:T(2,128)S(1)}, f32[2,73,720]{2,0,1:T(2,128)S(1)}, u32[]{:S(2)}, u32[]{:S(2)}) collective-permute-start(f32[2,73,720]{2,0,1:T(2,128)S(1)} %add.70), channel_id=1, source_target_pairs={{0,16},{8,24},{16,0},{24,8},{1,17},{9,25},{17,1},{25,9},{2,18},{10... | collective-permute-start | bytes 1261448 | tf_op jit(solution)/shard_map/ppermute | solution.py:63
Sparse Core Ops, SparseCore 0:
  9.5 33.4 all-gather.1
  96.2 71.3 all-reduce.1
